TPU v7x, 32 devices: a whole 2x2x4 slice. The times are simulated.
32 devices in a mesh: section: 4 (over x, core), ep: 8 (over z, y).
Axes of the slice: x: 2, y: 2, z: 4, core: 2. Of those that a mesh axis runs over, the one named last changes fastest.
Arguments:
- hidden_states: bfloat16 [384, 6144], P('ep'), may hold values from -6 to 6
- route_experts: int32 [384, 2], P('ep'), may hold values from 0 to 7, all different within a row; in each aligned block of 48 rows (0 to 47, 48 to 95, ...) at most 24 rows name the same one
- route_weights: float32 [384, 2], P('ep'), may hold values from 0.05 to 1
- gate_weight: bfloat16 [8, 6144, 8192], P('ep', None, 'section'), may hold values from -0.078125 to 0.078125
- up_weight: bfloat16 [8, 6144, 8192], P('ep', None, 'section'), may hold values from -0.078125 to 0.078125
- down_weight: bfloat16 [8, 8192, 6144], P('ep', 'section'), may hold values from -0.0625 to 0.0625
Outputs:
- layer_out: bfloat16 [384, 6144], P('ep', 'section')
Inputs may be any that keep to these rules, and one draw needn't show every extreme that they name: `route_experts`: each row names two different experts. Among the 48 rows of one ep index no expert is named by more than 24 rows, and in every draw some expert is named by exactly 24 rows of some ep index.
All inputs are finite; a program needn't handle non-finite values.
Results may differ from a plain program's by a relative error of at most 0.015.
Values may be sent and summed in bfloat16 or wider, within the bound.
A program may use at most 128 MiB of HBM per device.

v0:
```python
import jax
import jax.numpy as jnp
from jax import lax
from jax.sharding import PartitionSpec as P

EXPERTS = 8


def expert_rows(incoming, gate_weight, up_weight, down_weight):
    sources, slot_count, features = incoming.shape
    stacked = incoming.reshape(sources * slot_count, features)
    gate_value = jnp.dot(stacked, gate_weight[0], preferred_element_type=jnp.float32)
    up_value = jnp.dot(stacked, up_weight[0], preferred_element_type=jnp.float32)
    hidden = (jax.nn.silu(gate_value) * up_value).astype(jnp.bfloat16)
    result = jnp.dot(hidden, down_weight[0], preferred_element_type=jnp.float32).astype(
        jnp.bfloat16
    )
    return result.reshape(sources, slot_count, features)


def on_device(hidden_states, route_experts, route_weights, gate_weight, up_weight, down_weight):
    ep_count = lax.axis_size("ep")
    section_count = lax.axis_size("section")
    tok_rows, features = hidden_states.shape
    members = ep_count // EXPERTS
    capacity = tok_rows // 2
    chosen = route_experts.reshape(-1)
    one_hot = (chosen[:, None] == jnp.arange(EXPERTS, dtype=jnp.int32)[None, :]).astype(jnp.int32)
    earlier = jnp.cumsum(one_hot, axis=0) - one_hot
    slot_index = jnp.sum(earlier * one_hot, axis=1)
    position = (chosen * capacity + slot_index).reshape(tok_rows, 2)
    columns = jnp.arange(EXPERTS * capacity, dtype=jnp.int32)
    matches = position[:, :, None] == columns[None, None, :]
    select = jnp.sum(matches.astype(jnp.int32), axis=1).astype(jnp.bfloat16)
    weighing = jnp.sum(matches.astype(jnp.float32) * route_weights[:, :, None], axis=1)
    packed = jnp.einsum(
        "tj,td->jd", select, hidden_states, preferred_element_type=jnp.float32
    ).astype(jnp.bfloat16)
    outgoing = jnp.repeat(packed.reshape(EXPERTS, capacity, features), members, axis=0)
    slot_share = capacity // section_count
    first_slot = lax.axis_index("section") * slot_share
    own_slots = lax.dynamic_slice_in_dim(outgoing, first_slot, slot_share, 1)
    arrived = lax.all_to_all(own_slots, "ep", split_axis=0, concat_axis=0, tiled=True)
    partials = expert_rows(
        lax.all_gather(arrived, "section", axis=1, tiled=True), gate_weight, up_weight, down_weight
    )
    summed = lax.psum_scatter(
        partials.astype(jnp.float32).astype(jnp.bfloat16),
        "section",
        scatter_dimension=1,
        tiled=True,
    ).astype(jnp.float32)
    returned = lax.all_to_all(
        summed.astype(jnp.bfloat16), "ep", split_axis=0, concat_axis=0, tiled=True
    ).astype(summed.dtype)
    merged = jnp.sum(returned.reshape(EXPERTS, members, slot_share, features), axis=1)
    weigh_part = lax.dynamic_slice_in_dim(
        weighing.reshape(tok_rows, EXPERTS, capacity), first_slot, slot_share, 2
    )
    contribution = jnp.dot(
        weigh_part.reshape(tok_rows, EXPERTS * slot_share),
        merged.reshape(EXPERTS * slot_share, features),
        precision=lax.Precision.HIGHEST,
        preferred_element_type=jnp.float32,
    )
    layer_out = lax.psum_scatter(
        contribution.astype(jnp.bfloat16), "section", scatter_dimension=1, tiled=True
    )
    return layer_out


def solution(mesh):
    return jax.shard_map(
        on_device,
        mesh=mesh,
        in_specs=(
            P("ep", None),
            P("ep", None),
            P("ep", None),
            P("ep", None, "section"),
            P("ep", None, "section"),
            P("ep", "section", None),
        ),
        out_specs=P("ep", "section"),
        check_vma=False,
    )
```

profile of v0, /device:TPU:0, one launch (start us, length us, event | category | flops | bytes accessed | tf_op | source)
XLA Modules:
  0.0 190.9 jit_solution(7854758130795143767)
XLA Ops:
  6.5 0.8 copy.54
  7.4 0.1 eq.28
  7.5 0.1 fusion.25
  7.6 0.1 reduce_window_sum.11
  7.7 0.2 select_reduce_fusion.1
  7.9 0.1 reduce_sum.34
  8.0 0.1 copy.55
  8.1 0.7 multiply_add_fusion
  8.8 0.1 convert_reduce_fusion
  8.9 0.8 convolution_convert_fusion
  9.7 0.2 constant_dynamic-slice_fusion.1
  9.9 27.3 %all_to_all.10 = bf16[8,6,6144]{2,1,0:T(8,128)(2,1)S(1)} all-to-all(bf16[8,6,6144]{2,1,0:T(8,128)(2,1)S(1)} %constant_dynamic-slice_fusion.1), channel_id=1, replica_groups=mesh['section'=4,'ep'=8] {'ep'}, dimensions={0} | all-to-all | bytes 1179648 | tf_op jit(solution)/shard_map/all_to_all | solution.py:43
  37.2 1.2 copy.58
  38.4 0.0 all-gather.2.cloned.1.call-update
  38.4 0.0 reduce-scatter.3.cloned.1.call-start
  38.4 23.2 %all-gather.2.cloned.1.call-done = bf16[8,24,6144]{2,0,1:T(8,128)(2,1)} async-done(((bf16[8,6,6144]{2,0,1:T(8,128)(2,1)}), bf16[8,24,6144]{2,0,1:T(8,128)(2,1)}) %all-gather.2.cloned.1.call-update) | async-done | bytes 2359312 | tf_op jit(solution)/shard_map/all_gather | solution.py:45
  61.6 3.0 %copy.59 = bf16[8,24,6144]{2,1,0:T(8,128)(2,1)S(1)} copy(bf16[8,24,6144]{2,0,1:T(8,128)(2,1)} %all-gather.2.cloned.1.call-done) | data formatting | bytes 4718592 | tf_op jit(solution)/shard_map/all_gather | solution.py:45
  64.6 12.0 %fusion.4 = f32[192,2048]{1,0:T(8,128)} fusion(bf16[192,6144]{1,0:T(8,128)(2,1)S(1)} %bitcast.29, bf16[1,6144,2048]{2,1,0:T(8,128)(2,1)} %param.9), kind=kOutput, calls=%fused_computation.4 | convolution fusion | flops 4831838208 | bytes 29097984 | tf_op jit(solution)/shard_map/dot_general | solution.py:12
  76.5 20.7 %fusion.6 = bf16[192,6144]{1,0:T(8,128)(2,1)} fusion(bf16[1,2048,6144]{2,1,0:T(8,128)(2,1)} %param.11, bf16[192,6144]{1,0:T(8,128)(2,1)S(1)} %bitcast.30, bf16[1,6144,2048]{2,1,0:T(8,128)(2,1)} %param.10, f32[192,2048]{1,0:T(8,128)} %fusion.4), kind=kOutput, calls=%fused_computation.6 | convolution fusion | flops 9667215360 | bytes 56623104 | tf_op jit(solution)/shard_map/dot_general | solution.py:15
  97.3 4.4 %copy.60 = bf16[8,24,6144]{2,0,1:T(8,128)(2,1)} copy(bf16[8,24,6144]{2,1,0:T(8,128)(2,1)} %bitcast.31) | data formatting | bytes 4718592 | tf_op jit(solution)/shard_map/reshape | solution.py:18
  101.6 0.0 reduce-scatter.3.cloned.1.call-update
  101.7 0.0 copy-start.1
  101.7 33.0 %reduce-scatter.3.cloned.1.call-done = bf16[8,6,6144]{2,0,1:T(8,128)(2,1)} async-done(((bf16[8,24,6144]{2,0,1:T(8,128)(2,1)}), bf16[8,6,6144]{2,0,1:T(8,128)(2,1)}) %reduce-scatter.3.cloned.1.call-update) | async-done | bytes 589840 | tf_op jit(solution)/shard_map/reduce_scatter | solution.py:47
  134.6 2.3 %copy.61 = bf16[8,6,6144]{2,1,0:T(8,128)(2,1)} copy(bf16[8,6,6144]{2,0,1:T(8,128)(2,1)} %reduce-scatter.3.cloned.1.call-done) | data formatting | bytes 1179648 | tf_op jit(solution)/shard_map/reduce_scatter | solution.py:47
  136.9 5.5 %all-to-all-start.1 = ((bf16[8,6,6144]{2,1,0:T(8,128)(2,1)}), bf16[8,6,6144]{2,1,0:T(8,128)(2,1)S(1)}, u32[]{:S(2)}, u32[]{:S(2)}) async-start(bf16[8,6,6144]{2,1,0:T(8,128)(2,1)} %copy.61), calls=%async_computation.2 | async-start | bytes 1572864 | tf_op jit(solution)/shard_map/all_to_all | solution.py:53
  142.4 0.0 reduce-scatter.5.cloned.1.call-start
  142.5 0.1 select_reduce_fusion
  142.6 0.1 copy.56
  142.7 19.8 %all-to-all-done.1 = bf16[8,6,6144]{2,1,0:T(8,128)(2,1)S(1)} async-done(((bf16[8,6,6144]{2,1,0:T(8,128)(2,1)}), bf16[8,6,6144]{2,1,0:T(8,128)(2,1)S(1)}, u32[]{:S(2)}, u32[]{:S(2)}) %all-to-all-start.1) | async-done | bytes 589856 | tf_op jit(solution)/shard_map/all_to_all | solution.py:53
  162.5 1.7 fusion.9
  164.2 0.0 reduce-scatter.5.cloned.1.call-update
  164.2 20.2 %reduce-scatter.5.cloned.1.call-done = bf16[48,1536]{1,0:T(8,128)(2,1)} async-done(((bf16[48,6144]{1,0:T(8,128)(2,1)}), bf16[48,1536]{1,0:T(8,128)(2,1)}) %reduce-scatter.5.cloned.1.call-update) | async-done | bytes 147472 | tf_op jit(solution)/shard_map/reduce_scatter | solution.py:66
  (7 shorter events, 0.0 us)
Async XLA Ops:
  6.5 2.4 %copy-start = (bf16[48,6144]{1,0:T(8,128)(2,1)S(1)}, bf16[48,6144]{1,0:T(8,128)(2,1)}, u32[]{:S(2)}) copy-start(bf16[48,6144]{1,0:T(8,128)(2,1)} %param.6) | copy-start | bytes 1769476
  6.5 55.1 %all-gather.2.cloned.1.call-start = ((), (), s32[]{:S(2)}) async-start(), calls=%async_computation.4 | async-start | bytes 2949120 | tf_op jit(solution)/shard_map/all_gather | solution.py:45
  38.4 96.3 %reduce-scatter.3.cloned.1.call-start = ((), (), s32[]{:S(2)}) async-start(), calls=%async_computation.5 | async-start | bytes 2949120 | tf_op jit(solution)/shard_map/reduce_scatter | solution.py:47
  101.6 40.8 %copy-start.2 = (f32[48,2]{0,1:T(2,128)S(1)}, f32[48,2]{0,1:T(2,128)}, u32[]{:S(2)}) copy-start(f32[48,2]{0,1:T(2,128)} %param.8) | copy-start | bytes 1156
  101.7 82.7 %copy-start.1 = (bf16[48,6144]{1,0:T(8,128)(2,1)S(1)}, bf16[48,6144]{1,0:T(8,128)(2,1)}, u32[]{:S(2)}) copy-start(bf16[48,6144]{1,0:T(8,128)(2,1)} %param.6) | copy-start | bytes 1769476
  136.9 25.6 %all-to-all-start.1 = ((bf16[8,6,6144]{2,1,0:T(8,128)(2,1)}), bf16[8,6,6144]{2,1,0:T(8,128)(2,1)S(1)}, u32[]{:S(2)}, u32[]{:S(2)}) async-start(bf16[8,6,6144]{2,1,0:T(8,128)(2,1)} %copy.61), calls=%async_computation.2 | async-start | bytes 1572864 | tf_op jit(solution)/shard_map/all_to_all | solution.py:53
  142.4 42.0 %reduce-scatter.5.cloned.1.call-start = ((), (), s32[]{:S(2)}) async-start(), calls=%async_computation.6 | async-start | bytes 737280 | tf_op jit(solution)/shard_map/reduce_scatter | solution.py:66
Sparse Core Ops, SparseCore 0:
  38.5 23.0 all-gather.1
  101.8 32.8 reduce-scatter.2
  164.4 20.0 reduce-scatter.4
where the time goes:
time: 191 us
  waiting for transfers between devices  96.1 us (50%)
  matrix products  35.2 us (18%)
  blocking collectives  27.3 us (14%)
  between operations  13.2 us (7%)
  local copies, waits for them, and re-layouts  12.3 us (6%)
  starting transfers between devices  5.6 us (3%)
    reduce_scatter x1, waiting for transfers between devices, on_device(): lax.psum_scatter(partials.astype(jnp.float32).astype(jnp.bfloat16), 'sect...  33 us
    all_to_all x1, blocking collectives, on_device(): lax.all_to_all(own_slots, 'ep', split_axis=0, concat_axis=0, tiled=True)  27.3 us
    all_gather x1, waiting for transfers between devices, on_device(): lax.all_gather(arrived, 'section', axis=1, tiled=True)  23.2 us
    dot_general x1, matrix products, expert_rows(): jnp.dot(hidden, down_weight[0], preferred_element_type=jnp.float32)  20.7 us
    reduce_scatter x1, waiting for transfers between devices, on_device(): lax.psum_scatter(contribution.astype(jnp.bfloat16), 'section', scatter_di...  20.2 us
    all_to_all x1, waiting for transfers between devices, on_device(): lax.all_to_all(summed.astype(jnp.bfloat16), 'ep', split_axis=0, concat_ax...  19.8 us
    dot_general x1, matrix products, expert_rows(): jnp.dot(stacked, gate_weight[0], preferred_element_type=jnp.float32)  12 us
    all_to_all x1, starting transfers between devices, on_device(): lax.all_to_all(summed.astype(jnp.bfloat16), 'ep', split_axis=0, concat_ax...  5.52 us
  transfers between devices with their start and end apart: 4, of which 4 were waited for; matrix products, arithmetic and copies ran while one was open for 0% of the time, Pallas kernels for 0%

commit v1 on v0

--- a/solution.py
+++ b/solution.py
@@ -4,6 +4,22 @@
 from jax.sharding import PartitionSpec as P
 
 EXPERTS = 8
+
+
+def exchange_in_pairs(x, axis, split, join):
+    ways, here = (lax.axis_size(axis), lax.axis_index(axis))
+    width = x.shape[split] // ways
+    shape = list(x.shape)
+    shape[split] = width
+    height = shape[join]
+    shape[join] = height * ways
+    full = jnp.zeros(shape, x.dtype)
+    for mask in range(ways):
+        part = lax.dynamic_slice_in_dim(x, (here ^ mask) * width, width, axis=split)
+        if mask:
+            part = lax.ppermute(part, axis, [(d, d ^ mask) for d in range(ways)])
+        full = lax.dynamic_update_slice_in_dim(full, part, (here ^ mask) * height, axis=join)
+    return full
 
 
 def expert_rows(incoming, gate_weight, up_weight, down_weight):
@@ -40,7 +56,7 @@
     slot_share = capacity // section_count
     first_slot = lax.axis_index("section") * slot_share
     own_slots = lax.dynamic_slice_in_dim(outgoing, first_slot, slot_share, 1)
-    arrived = lax.all_to_all(own_slots, "ep", split_axis=0, concat_axis=0, tiled=True)
+    arrived = exchange_in_pairs(own_slots, "ep", 0, 0)
     partials = expert_rows(
         lax.all_gather(arrived, "section", axis=1, tiled=True), gate_weight, up_weight, down_weight
     )

time: 191 us -> 200 us (1.047)
  blocking collectives: 27.3 us -> 0 us
  starting transfers between devices: 5.6 us -> 18.9 us
  local copies, waits for them, and re-layouts: 12.3 us -> 24.5 us
  waiting for transfers between devices: 96.1 us -> 106 us
    all_to_all x1 -> x0, blocking collectives: 27.3 us -> none  [on_device(): lax.all_to_all(own_slots, 'ep', split_axis=0, concat_axis=0, tiled=True)]
    ppermute x0 -> x7, starting transfers between devices: none -> 13.1 us  [exchange_in_pairs(): part = lax.ppermute(part, axis, [(d, d ^ mask) for d in range(ways)])]
    dynamic_update_slice x0 -> x8, local copies, waits for them, and re-layouts: none -> 11.6 us  [exchange_in_pairs(): lax.dynamic_update_slice_in_dim(full, part, (here ^ mask) * height, axis=...]
    ppermute x0 -> x7, waiting for transfers between devices: none -> 8.18 us  [exchange_in_pairs(): part = lax.ppermute(part, axis, [(d, d ^ mask) for d in range(ways)])]
    all_gather x1, waiting for transfers between devices: 23.2 us -> 25.3 us  [on_device(): lax.all_gather(arrived, 'section', axis=1, tiled=True)]
  transfers between devices with their start and end apart: 4 -> 11, of which waited for: 4 -> 6; matrix products, arithmetic and copies ran while one was open for 0% -> 6% of each run, Pallas kernels for 0% -> 0%
where the time goes in v1:
time: 200 us
  waiting for transfers between devices  106 us (53%)
  matrix products  35.2 us (18%)
  local copies, waits for them, and re-layouts  24.5 us (12%)
  starting transfers between devices  18.9 us (9%)
  between operations  13.4 us (7%)
    reduce_scatter x1, waiting for transfers between devices, on_device(): lax.psum_scatter(partials.astype(jnp.float32).astype(jnp.bfloat16), 'sect...  33 us
    all_gather x1, waiting for transfers between devices, on_device(): lax.all_gather(arrived, 'section', axis=1, tiled=True)  25.3 us
    dot_general x1, matrix products, expert_rows(): jnp.dot(hidden, down_weight[0], preferred_element_type=jnp.float32)  20.7 us
    reduce_scatter x1, waiting for transfers between devices, on_device(): lax.psum_scatter(contribution.astype(jnp.bfloat16), 'section', scatter_di...  20.2 us
    all_to_all x1, waiting for transfers between devices, on_device(): lax.all_to_all(summed.astype(jnp.bfloat16), 'ep', split_axis=0, concat_ax...  19.8 us
    ppermute x7, starting transfers between devices, exchange_in_pairs(): part = lax.ppermute(part, axis, [(d, d ^ mask) for d in range(ways)])  13.1 us
    dot_general x1, matrix products, expert_rows(): jnp.dot(stacked, gate_weight[0], preferred_element_type=jnp.float32)  12 us
    dynamic_update_slice x8, local copies, waits for them, and re-layouts, exchange_in_pairs(): lax.dynamic_update_slice_in_dim(full, part, (here ^ mask) * height, axis=...  11.6 us
  transfers between devices with their start and end apart: 11, of which 6 were waited for; matrix products, arithmetic and copies ran while one was open for 6% of the time, Pallas kernels for 0%

profile of v1, /device:TPU:0, one launch (start us, length us, event | category | flops | bytes accessed | tf_op | source)
XLA Modules:
  0.0 199.7 jit_solution(2322719364169840151)
XLA Ops:
  6.5 0.8 copy.82
  8.1 0.7 multiply_add_fusion
  8.9 0.8 convolution_convert_fusion
  9.7 0.3 constant_dynamic-slice_fusion
  10.1 3.1 %collective-permute-start = (bf16[1,6,6144]{2,0,1:T(2,128)(2,1)S(1)}, bf16[1,6,6144]{2,0,1:T(2,128)(2,1)S(1)}, u32[]{:S(2)}, u32[]{:S(2)}) collective-permute-start(bf16[1,6,6144]{2,0,1:T(2,128)(2,1)S(1)} %copy.100), channel_id=1, source_target_pairs={{0,1},{1,0},{2,3},{3,2},{4,5},{5,4},{6,7},{7,6},{8,9},{9,8},{10,11... | collective-permute-start | bytes 221192 | tf_op jit(solution)/shard_map/ppermute | solution.py:20
  13.3 1.6 collective-permute-start.1
  15.3 3.0 %collective-permute-start.3 = (bf16[1,6,6144]{2,0,1:T(2,128)(2,1)S(1)}, bf16[1,6,6144]{2,0,1:T(2,128)(2,1)S(1)}, u32[]{:S(2)}, u32[]{:S(2)}) collective-permute-start(bf16[1,6,6144]{2,0,1:T(2,128)(2,1)S(1)} %copy.103), channel_id=1, source_target_pairs={{0,4},{1,5},{2,6},{3,7},{4,0},{5,1},{6,2},{7,3},{8,12},{9,13},{10,... | collective-permute-start | bytes 221192 | tf_op jit(solution)/shard_map/ppermute | solution.py:20
  18.4 1.4 collective-permute-start.4
  20.0 3.7 %collective-permute-start.5 = (bf16[1,6,6144]{2,0,1:T(2,128)(2,1)S(1)}, bf16[1,6,6144]{2,0,1:T(2,128)(2,1)S(1)}, u32[]{:S(2)}, u32[]{:S(2)}) collective-permute-start(bf16[1,6,6144]{2,0,1:T(2,128)(2,1)S(1)} %copy.105), channel_id=1, source_target_pairs={{0,6},{1,7},{2,4},{3,5},{4,2},{5,3},{6,0},{7,1},{8,14},{9,15},{10,... | collective-permute-start | bytes 221192 | tf_op jit(solution)/shard_map/ppermute | solution.py:20
  23.7 1.5 collective-permute-done.1
  25.1 0.3 collective-permute-start.6
  25.6 1.5 dynamic_update_slice.24
  27.0 1.5 dynamic_update_slice.25
  28.5 1.5 dynamic_update_slice.26
  30.0 1.5 dynamic_update_slice.27
  31.4 1.5 dynamic_update_slice.28
  32.9 6.7 %collective-permute-done.4 = bf16[1,6,6144]{2,0,1:T(2,128)(2,1)S(1)} collective-permute-done((bf16[1,6,6144]{2,0,1:T(2,128)(2,1)S(1)}, bf16[1,6,6144]{2,0,1:T(2,128)(2,1)S(1)}, u32[]{:S(2)}, u32[]{:S(2)}) %collective-permute-start.4) | collective-permute-done | bytes 73760 | tf_op jit(solution)/shard_map/ppermute | solution.py:20
  39.6 1.4 dynamic_update_slice.29
  41.0 1.5 dynamic_update_slice.30
  42.5 1.5 dynamic_update_slice.31
  44.0 0.8 copy-done.2
  45.0 25.3 %all-gather.2.cloned.1.call-done = bf16[8,24,6144]{2,0,1:T(8,128)(2,1)} async-done(((bf16[8,6,6144]{2,0,1:T(8,128)(2,1)}), bf16[8,24,6144]{2,0,1:T(8,128)(2,1)}) %all-gather.2.cloned.1.call-update) | async-done | bytes 2359312 | tf_op jit(solution)/shard_map/all_gather | solution.py:61
  70.3 3.0 %copy.94 = bf16[8,24,6144]{2,1,0:T(8,128)(2,1)S(1)} copy(bf16[8,24,6144]{2,0,1:T(8,128)(2,1)} %all-gather.2.cloned.1.call-done) | data formatting | bytes 4718592 | tf_op jit(solution)/shard_map/all_gather | solution.py:61
  73.3 12.0 %fusion.4 = f32[192,2048]{1,0:T(8,128)} fusion(bf16[192,6144]{1,0:T(8,128)(2,1)S(1)} %bitcast.29, bf16[1,6144,2048]{2,1,0:T(8,128)(2,1)} %param.9), kind=kOutput, calls=%fused_computation.4 | convolution fusion | flops 4831838208 | bytes 29097984 | tf_op jit(solution)/shard_map/dot_general | solution.py:28
  85.2 20.7 %fusion.6 = bf16[192,6144]{1,0:T(8,128)(2,1)} fusion(bf16[1,2048,6144]{2,1,0:T(8,128)(2,1)} %param.11, bf16[192,6144]{1,0:T(8,128)(2,1)S(1)} %bitcast.30, bf16[1,6144,2048]{2,1,0:T(8,128)(2,1)} %param.10, f32[192,2048]{1,0:T(8,128)} %fusion.4), kind=kOutput, calls=%fused_computation.6 | convolution fusion | flops 9667215360 | bytes 56623104 | tf_op jit(solution)/shard_map/dot_general | solution.py:31
  106.0 4.4 %copy.95 = bf16[8,24,6144]{2,0,1:T(8,128)(2,1)} copy(bf16[8,24,6144]{2,1,0:T(8,128)(2,1)} %bitcast.31) | data formatting | bytes 4718592 | tf_op jit(solution)/shard_map/reshape | solution.py:34
  110.4 33.0 %reduce-scatter.3.cloned.1.call-done = bf16[8,6,6144]{2,0,1:T(8,128)(2,1)} async-done(((bf16[8,24,6144]{2,0,1:T(8,128)(2,1)}), bf16[8,6,6144]{2,0,1:T(8,128)(2,1)}) %reduce-scatter.3.cloned.1.call-update) | async-done | bytes 589840 | tf_op jit(solution)/shard_map/reduce_scatter | solution.py:63
  143.3 2.3 %copy.96 = bf16[8,6,6144]{2,1,0:T(8,128)(2,1)} copy(bf16[8,6,6144]{2,0,1:T(8,128)(2,1)} %reduce-scatter.3.cloned.1.call-done) | data formatting | bytes 1179648 | tf_op jit(solution)/shard_map/reduce_scatter | solution.py:63
  145.6 5.5 %all-to-all-start = ((bf16[8,6,6144]{2,1,0:T(8,128)(2,1)}), bf16[8,6,6144]{2,1,0:T(8,128)(2,1)S(1)}, u32[]{:S(2)}, u32[]{:S(2)}) async-start(bf16[8,6,6144]{2,1,0:T(8,128)(2,1)} %copy.96), calls=%async_computation.1 | async-start | bytes 1572864 | tf_op jit(solution)/shard_map/all_to_all | solution.py:69
  151.4 19.8 %all-to-all-done = bf16[8,6,6144]{2,1,0:T(8,128)(2,1)S(1)} async-done(((bf16[8,6,6144]{2,1,0:T(8,128)(2,1)}), bf16[8,6,6144]{2,1,0:T(8,128)(2,1)S(1)}, u32[]{:S(2)}, u32[]{:S(2)}) %all-to-all-start) | async-done | bytes 589856 | tf_op jit(solution)/shard_map/all_to_all | solution.py:69
  171.2 1.7 fusion.9
  173.0 20.2 %reduce-scatter.5.cloned.1.call-done = bf16[48,1536]{1,0:T(8,128)(2,1)} async-done(((bf16[48,6144]{1,0:T(8,128)(2,1)}), bf16[48,1536]{1,0:T(8,128)(2,1)}) %reduce-scatter.5.cloned.1.call-update) | async-done | bytes 147472 | tf_op jit(solution)/shard_map/reduce_scatter | solution.py:82
  (38 shorter events, 2.4 us)
Async XLA Ops:
  6.5 2.4 %copy-start = (bf16[48,6144]{1,0:T(8,128)(2,1)S(1)}, bf16[48,6144]{1,0:T(8,128)(2,1)}, u32[]{:S(2)}) copy-start(bf16[48,6144]{1,0:T(8,128)(2,1)} %param.6) | copy-start | bytes 1769476
  6.5 63.8 %all-gather.2.cloned.1.call-start = ((), (), s32[]{:S(2)}) async-start(), calls=%async_computation.3 | async-start | bytes 2949120 | tf_op jit(solution)/shard_map/all_gather | solution.py:61
  10.1 9.9 %collective-permute-start = (bf16[1,6,6144]{2,0,1:T(2,128)(2,1)S(1)}, bf16[1,6,6144]{2,0,1:T(2,128)(2,1)S(1)}, u32[]{:S(2)}, u32[]{:S(2)}) collective-permute-start(bf16[1,6,6144]{2,0,1:T(2,128)(2,1)S(1)} %copy.100), channel_id=1, source_target_pairs={{0,1},{1,0},{2,3},{3,2},{4,5},{5,4},{6,7},{7,6},{8,9},{9,8},{10,11... | collective-permute-start | bytes 221192 | tf_op jit(solution)/shard_map/ppermute | solution.py:20
  13.3 11.8 %collective-permute-start.1 = (bf16[1,6,6144]{2,0,1:T(2,128)(2,1)S(1)}, bf16[1,6,6144]{2,0,1:T(2,128)(2,1)S(1)}, u32[]{:S(2)}, u32[]{:S(2)}) collective-permute-start(bf16[1,6,6144]{2,0,1:T(2,128)(2,1)S(1)} %copy.101), channel_id=1, source_target_pairs={{0,2},{1,3},{2,0},{3,1},{4,6},{5,7},{6,4},{7,5},{8,10},{9,11},{10,... | collective-permute-start | bytes 221192 | tf_op jit(solution)/shard_map/ppermute | solution.py:20
  15.0 14.9 %collective-permute-start.2 = (bf16[1,6,6144]{2,0,1:T(2,128)(2,1)S(1)}, bf16[1,6,6144]{2,0,1:T(2,128)(2,1)S(1)}, u32[]{:S(2)}, u32[]{:S(2)}) collective-permute-start(bf16[1,6,6144]{2,0,1:T(2,128)(2,1)S(1)} %copy.102), channel_id=1, source_target_pairs={{0,3},{1,2},{2,1},{3,0},{4,7},{5,6},{6,5},{7,4},{8,11},{9,10},{10,... | collective-permute-start | bytes 221192 | tf_op jit(solution)/shard_map/ppermute | solution.py:20
  15.3 16.2 %collective-permute-start.3 = (bf16[1,6,6144]{2,0,1:T(2,128)(2,1)S(1)}, bf16[1,6,6144]{2,0,1:T(2,128)(2,1)S(1)}, u32[]{:S(2)}, u32[]{:S(2)}) collective-permute-start(bf16[1,6,6144]{2,0,1:T(2,128)(2,1)S(1)} %copy.103), channel_id=1, source_target_pairs={{0,4},{1,5},{2,6},{3,7},{4,0},{5,1},{6,2},{7,3},{8,12},{9,13},{10,... | collective-permute-start | bytes 221192 | tf_op jit(solution)/shard_map/ppermute | solution.py:20
  18.4 21.2 %collective-permute-start.4 = (bf16[1,6,6144]{2,0,1:T(2,128)(2,1)S(1)}, bf16[1,6,6144]{2,0,1:T(2,128)(2,1)S(1)}, u32[]{:S(2)}, u32[]{:S(2)}) collective-permute-start(bf16[1,6,6144]{2,0,1:T(2,128)(2,1)S(1)} %copy.104), channel_id=1, source_target_pairs={{0,5},{1,4},{2,7},{3,6},{4,1},{5,0},{6,3},{7,2},{8,13},{9,12},{10,... | collective-permute-start | bytes 221192 | tf_op jit(solution)/shard_map/ppermute | solution.py:20
  20.0 21.0 %collective-permute-start.5 = (bf16[1,6,6144]{2,0,1:T(2,128)(2,1)S(1)}, bf16[1,6,6144]{2,0,1:T(2,128)(2,1)S(1)}, u32[]{:S(2)}, u32[]{:S(2)}) collective-permute-start(bf16[1,6,6144]{2,0,1:T(2,128)(2,1)S(1)} %copy.105), channel_id=1, source_target_pairs={{0,6},{1,7},{2,4},{3,5},{4,2},{5,3},{6,0},{7,1},{8,14},{9,15},{10,... | collective-permute-start | bytes 221192 | tf_op jit(solution)/shard_map/ppermute | solution.py:20
  25.1 17.4 %collective-permute-start.6 = (bf16[1,6,6144]{2,0,1:T(2,128)(2,1)S(1)}, bf16[1,6,6144]{2,0,1:T(2,128)(2,1)S(1)}, u32[]{:S(2)}, u32[]{:S(2)}) collective-permute-start(bf16[1,6,6144]{2,0,1:T(2,128)(2,1)S(1)} %copy.106), channel_id=1, source_target_pairs={{0,7},{1,6},{2,5},{3,4},{4,3},{5,2},{6,1},{7,0},{8,15},{9,14},{10,... | collective-permute-start | bytes 221192 | tf_op jit(solution)/shard_map/ppermute | solution.py:20
  44.0 0.8 copy-start.2
  44.8 98.5 %reduce-scatter.3.cloned.1.call-start = ((), (), s32[]{:S(2)}) async-start(), calls=%async_computation.4 | async-start | bytes 2949120 | tf_op jit(solution)/shard_map/reduce_scatter | solution.py:63
  110.4 40.9 %copy-start.3 = (f32[48,2]{0,1:T(2,128)S(1)}, f32[48,2]{0,1:T(2,128)}, u32[]{:S(2)}) copy-start(f32[48,2]{0,1:T(2,128)} %param.8) | copy-start | bytes 1156
  110.4 82.8 %copy-start.1 = (bf16[48,6144]{1,0:T(8,128)(2,1)S(1)}, bf16[48,6144]{1,0:T(8,128)(2,1)}, u32[]{:S(2)}) copy-start(bf16[48,6144]{1,0:T(8,128)(2,1)} %param.6) | copy-start | bytes 1769476
  145.6 25.6 %all-to-all-start = ((bf16[8,6,6144]{2,1,0:T(8,128)(2,1)}), bf16[8,6,6144]{2,1,0:T(8,128)(2,1)S(1)}, u32[]{:S(2)}, u32[]{:S(2)}) async-start(bf16[8,6,6144]{2,1,0:T(8,128)(2,1)} %copy.96), calls=%async_computation.1 | async-start | bytes 1572864 | tf_op jit(solution)/shard_map/all_to_all | solution.py:69
  151.2 42.0 %reduce-scatter.5.cloned.1.call-start = ((), (), s32[]{:S(2)}) async-start(), calls=%async_computation.5 | async-start | bytes 737280 | tf_op jit(solution)/shard_map/reduce_scatter | solution.py:82
Sparse Core Ops, SparseCore 0:
  44.9 25.3 all-gather.1
  110.5 32.8 reduce-scatter.2
  173.1 20.0 reduce-scatter.4
